TPU v7x, 32 devices: a whole 2x2x4 slice. The times are simulated.
32 devices in a mesh: ha: 2 (over x), vert: 16 (over z, y, core).
Axes of the slice: x: 2, y: 2, z: 4, core: 2. Of those that a mesh axis runs over, the one named last changes fastest.
Arguments:
- hidden: bfloat16 [128, 16384], P('vert', 'ha'), may hold values from -6 to 6
- norm_gain: float32 [16384], P('ha'), may hold values from 0.25 to 1.75
- head_weight: bfloat16 [16384, 32064], P('ha', 'vert'), may hold values from -0.046875 to 0.046875
- targets: int32 [128], replicated, may hold values from 0 to 32063
Outputs:
- log_probs: float32 [128, 32064], P('ha', 'vert')
- target_logprob: float32 [128], P('ha')
Inputs may be any that keep to these rules, and one draw needn't show every extreme that they name: `targets`: every next token id lies in 0 to 32063.
All inputs are finite; a program needn't handle non-finite values.
Results may differ from a plain program's by a relative error of at most 0.0015.
Values may be sent and summed in bfloat16 or wider, within the bound.
A program may use at most 64 MiB of HBM per device.

v0:
```python
import jax
import jax.numpy as jnp
from jax import lax
from jax.sharding import PartitionSpec as P

D = 16384


def combined_all(part, axis, combine):
    gathered = jax.tree.map(lambda a: lax.all_gather(a, axis), part)

    def take(source):
        return jax.tree.map(lambda a: lax.dynamic_index_in_dim(a, source, 0, False), gathered)

    return lax.fori_loop(
        1, lax.axis_size(axis), lambda source, state: combine(state, take(source)), take(0)
    )


def combine(earlier, later_one):
    largest = jnp.maximum(earlier[0], later_one[0])
    expsum = earlier[1] * jnp.exp(earlier[0] - largest) + later_one[1] * jnp.exp(
        later_one[0] - largest
    )
    return (largest, expsum, earlier[2] + later_one[2])


def shards(hidden, norm_gain, head_weight, targets):
    vocab_width = head_weight.shape[1]
    vocab_start = lax.axis_index("vert") * vocab_width
    ha_count = lax.axis_size("ha")
    batch_total = hidden.shape[0] * lax.axis_size("vert")
    own_rows = batch_total // ha_count

    def partial_terms(block_rows):
        widened = block_rows.astype(jnp.float32)
        scaled = (widened * norm_gain[None, :]).astype(jnp.bfloat16)
        product = jnp.dot(scaled, head_weight, preferred_element_type=jnp.float32)
        squares = jnp.sum(widened * widened, axis=1, keepdims=True)
        return jnp.concatenate([product, squares], axis=1)

    def finish(summed, row_targets):
        unscaled = summed[:, :vocab_width]
        inverse = lax.rsqrt(summed[:, vocab_width:] / D + 1e-05)
        logits = unscaled * inverse
        local_max = jnp.max(logits, axis=1)
        local_sum = jnp.sum(jnp.exp(logits - local_max[:, None]), axis=1)
        columns = vocab_start + jnp.arange(vocab_width, dtype=jnp.int32)
        matches = row_targets[:, None] == columns[None, :]
        local_target = jnp.sum(jnp.where(matches, logits, 0.0), axis=1)
        largest, expsum, target_sum = combined_all(
            (local_max, local_sum, local_target), "vert", combine
        )
        log_total = largest + jnp.log(expsum)
        return (logits - log_total[:, None], target_sum - log_total)

    first_row = lax.axis_index("ha") * own_rows
    gathered = lax.all_gather(hidden, "vert", axis=0, tiled=True)
    summed = lax.psum_scatter(
        partial_terms(lax.slice_in_dim(gathered, 0, own_rows * lax.axis_size("ha"), axis=0)).astype(
            jnp.bfloat16
        ),
        "ha",
        scatter_dimension=0,
        tiled=True,
    ).astype(jnp.float32)
    row_targets = lax.dynamic_slice_in_dim(targets, first_row, own_rows, 0)
    log_probs, picked = finish(summed, row_targets)
    return (log_probs, picked)


def solution(mesh):
    placed = (P("vert", "ha"), P("ha"), P("ha", "vert"), P())
    return jax.shard_map(
        shards, mesh=mesh, in_specs=placed, out_specs=(P("ha", "vert"), P("ha")), check_vma=False
    )
```

profile of v0, /device:TPU:0, one launch (start us, length us, event | category | flops | bytes accessed | tf_op | source)
XLA Modules:
  0.0 159.8 jit_solution(11805804333639017836)
XLA Ops:
  7.2 0.0 all-gather.5.cloned.1.call-start
  7.2 0.7 all-gather.5.cloned.1.call-update
  7.9 0.0 reduce-scatter.4.cloned.1.call-start
  7.9 46.4 %all-gather.5.cloned.1.call-done = bf16[128,8192]{1,0:T(8,128)(2,1)} async-done(((bf16[8,8192]{1,0:T(8,128)(2,1)}), bf16[128,8192]{1,0:T(8,128)(2,1)}) %all-gather.5.cloned.1.call-update) | async-done | bytes 2097168 | tf_op jit(solution)/shard_map/all_gather | solution.py:58
  54.4 2.1 %fusion.8 = bf16[128]{0:T(256)(128)(2,1)S(1)} fusion(bf16[128,8192]{1,0:T(8,128)(2,1)} %all-gather.5.cloned.1.call-done), kind=kLoop, calls=%fused_computation.13 | loop fusion | flops 3145600 | bytes 2097408 | tf_op jit(solution)/shard_map/reduce_sum | solution.py:39
  56.4 0.0 copy-start
  56.4 0.0 copy-start.1
  56.5 14.9 %convolution_convert_fusion = bf16[128,2004]{0,1:T(8,128)(2,1)S(1)} fusion(bf16[8192,2004]{0,1:T(8,128)(2,1)} %param.8, bf16[128,8192]{1,0:T(8,128)(2,1)} %all-gather.5.cloned.1.call-done, f32[8192]{0:T(1024)} %param.7), kind=kOutput, calls=%fused_computation.14 | convolution fusion | flops 4206094848 | bytes 35476480 | tf_op jit(solution)/shard_map/dot_general | solution.py:38
  71.4 1.0 copy.8
  72.5 0.0 reduce-scatter.4.cloned.1.call-update
  72.5 0.0 copy-done
  72.5 0.1 dynamic_slice.45
  72.6 0.0 copy-done.1
  72.6 0.6 dynamic-slice
  73.9 12.1 %reduce-scatter.4.cloned.1.call-done = bf16[64,2005]{1,0:T(8,128)(2,1)} async-done(((bf16[128,2005]{1,0:T(8,128)(2,1)}), bf16[64,2005]{1,0:T(8,128)(2,1)}) %reduce-scatter.4.cloned.1.call-update) | async-done | bytes 256656
  86.0 1.2 copy.9
  87.3 0.1 convert_element_type.12
  87.4 0.3 fusion.12
  87.6 1.0 select_reduce_fusion
  88.6 0.2 dynamic-update-slice
  88.9 0.2 dynamic-update-slice.2
  89.1 0.2 dynamic-update-slice.1
  89.3 61.0 %all-reduce.3 = (f32[1024]{0:T(1024)S(1)}, f32[1024]{0:T(1024)S(1)}, f32[1024]{0:T(1024)S(1)}) all-reduce(f32[1024]{0:T(1024)S(1)} %dynamic-update-slice, f32[1024]{0:T(1024)S(1)} %dynamic-update-slice.1, f32[1024]{0:T(1024)S(1)} %dynamic-update-slice.2), channel_id=2, replica_groups=mesh['ha'=2,'vert'=16] {'vert'}, use_global_device_ids=true, to_apply=%add | all-reduce | flops 3072 | bytes 24576
  150.3 0.1 reshape.12
  150.4 0.1 reshape.13
  150.4 0.1 reshape.14
  150.5 0.7 while.19
  151.2 0.5 fusion.17
  151.7 0.1 fusion.11
  151.8 1.1 copy.7
  (24 shorter events, 0.5 us)
Async XLA Ops:
  7.2 47.2 %all-gather.5.cloned.1.call-start = ((), (), s32[]{:S(2)}) async-start(), calls=%async_computation.1 | async-start | bytes 2228224 | tf_op jit(solution)/shard_map/all_gather | solution.py:58
  7.9 78.1 %reduce-scatter.4.cloned.1.call-start = ((), (), s32[]{:S(2)}) async-start(), calls=%async_computation.2 | async-start | bytes 786432
  56.4 16.1 %copy-start = (s32[128]{0:T(128)S(1)}, s32[128]{0:T(128)}, u32[]{:S(2)}) copy-start(s32[128]{0:T(128)} %param.9) | copy-start | bytes 1540
  56.4 16.2 %copy-start.1 = (u32[32]{0:T(128)S(1)}, u32[32]{0:T(128)}, u32[]{:S(2)}) copy-start(u32[32]{0:T(128)} %constant.79) | copy-start | bytes 388
Sparse Core Ops, SparseCore 0:
  10.1 44.1 all-gather.4
  72.6 13.3 reduce-scatter.3
where the time goes:
time: 160 us
  blocking collectives  61 us (38%)
  waiting for transfers between devices  59.2 us (37%)
  matrix products  14.9 us (9%)
  between operations  14.8 us (9%)
  local copies, waits for them, and re-layouts  5.02 us (3%)
  other arithmetic  4.48 us (3%)
    unnamed x1, blocking collectives  61 us
    all_gather x1, waiting for transfers between devices, shards(): gathered = lax.all_gather(hidden, 'vert', axis=0, tiled=True)  46.4 us
    dot_general x1, matrix products, partial_terms(): product = jnp.dot(scaled, head_weight, preferred_element_type=jnp.float32)  14.9 us
    unnamed x3, waiting for transfers between devices  12.8 us
    unnamed x14, local copies, waits for them, and re-layouts  4.73 us
  transfers between devices with their start and end apart: 2, of which 2 were waited for; matrix products, arithmetic and copies ran while one was open for 0% of the time, Pallas kernels for 0%

commit v1 on v0

--- a/solution.py
+++ b/solution.py
@@ -1,9 +1,27 @@
+import functools
 import jax
 import jax.numpy as jnp
 from jax import lax
 from jax.sharding import PartitionSpec as P
 
 D = 16384
+
+
+def balance_samples(frame_in, dev_axis):
+    n_all = lax.axis_size(dev_axis)
+    passed = sorted(((rr, (rr + 1) % n_all) for rr in range(n_all)))
+    u_next = frame_in
+    stack_in = [u_next]
+    dd = 1
+    while dd < n_all:
+        u_next = lax.ppermute(u_next, dev_axis, passed)
+        stack_in.insert(0, u_next)
+        dd += 1
+    reply = jnp.concatenate(stack_in, 0)
+    return jnp.roll(reply, (lax.axis_index(dev_axis) + 1) * frame_in.shape[0], 0)
+
+
+divide_the_quotas = functools.partial(balance_samples, dev_axis="vert")
 
 
 def combined_all(part, axis, combine):
@@ -55,7 +73,7 @@
         return (logits - log_total[:, None], target_sum - log_total)
 
     first_row = lax.axis_index("ha") * own_rows
-    gathered = lax.all_gather(hidden, "vert", axis=0, tiled=True)
+    gathered = divide_the_quotas(hidden)
     summed = lax.psum_scatter(
         partial_terms(lax.slice_in_dim(gathered, 0, own_rows * lax.axis_size("ha"), axis=0)).astype(
             jnp.bfloat16

time: 160 us -> 219 us (1.37)
  waiting for transfers between devices: 59.2 us -> 118 us
    ppermute x0 -> x15, waiting for transfers between devices: none -> 107 us  [balance_samples(): u_next = lax.ppermute(u_next, dev_axis, passed)]
    all_gather x1 -> x0, waiting for transfers between devices: 46.4 us -> none  [shards(): gathered = lax.all_gather(hidden, 'vert', axis=0, tiled=True)]
    unnamed x3 -> x2, waiting for transfers between devices: 12.8 us -> 11 us
    unnamed x14 -> x49, local copies, waits for them, and re-layouts: 4.73 us -> 6.01 us
  transfers between devices with their start and end apart: 2 -> 16, of which waited for: 2 -> 16; matrix products, arithmetic and copies ran while one was open for 0% -> 0% of each run, Pallas kernels for 0% -> 0%
where the time goes in v1:
time: 219 us; the launch traced here: 218 us
  waiting for transfers between devices  118 us (54%)
  blocking collectives  61 us (28%)
  between operations  15.1 us (7%)
  matrix products  14.1 us (6%)
  local copies, waits for them, and re-layouts  6.31 us (3%)
  other arithmetic  2.9 us (1%)
    ppermute x15, waiting for transfers between devices, balance_samples(): u_next = lax.ppermute(u_next, dev_axis, passed)  107 us
    unnamed x1, blocking collectives  61 us
    dot_general x1, matrix products, partial_terms(): product = jnp.dot(scaled, head_weight, preferred_element_type=jnp.float32)  14.1 us
    unnamed x2, waiting for transfers between devices  11 us
    unnamed x49, local copies, waits for them, and re-layouts  6.01 us
  transfers between devices with their start and end apart: 16, of which 16 were waited for; matrix products, arithmetic and copies ran while one was open for 0% of the time, Pallas kernels for 0%

profile of v1, /device:TPU:0, one launch (start us, length us, event | category | flops | bytes accessed | tf_op | source)
XLA Modules:
  0.0 218.4 jit_solution(3620379497404247836)
XLA Ops:
  7.2 0.0 copy-start
  7.2 0.0 reduce-scatter.4.cloned.1.call-start
  7.2 0.5 collective-permute-start
  7.8 7.8 %collective-permute-done = bf16[8,8192]{1,0:T(8,128)(2,1)S(1)} collective-permute-done((bf16[8,8192]{1,0:T(8,128)(2,1)}, bf16[8,8192]{1,0:T(8,128)(2,1)S(1)}, u32[]{:S(2)}, u32[]{:S(2)}) %collective-permute-start) | collective-permute-done | bytes 131104 | tf_op jit(solution)/shard_map/ppermute | solution.py:17
  15.6 0.0 collective-permute-start.1
  15.6 7.1 %collective-permute-done.1 = bf16[8,8192]{1,0:T(8,128)(2,1)S(1)} collective-permute-done((bf16[8,8192]{1,0:T(8,128)(2,1)S(1)}, bf16[8,8192]{1,0:T(8,128)(2,1)S(1)}, u32[]{:S(2)}, u32[]{:S(2)}) %collective-permute-start.1) | collective-permute-done | bytes 131104 | tf_op jit(solution)/shard_map/ppermute | solution.py:17
  22.7 0.0 collective-permute-start.2
  22.7 7.1 %collective-permute-done.2 = bf16[8,8192]{1,0:T(8,128)(2,1)S(1)} collective-permute-done((bf16[8,8192]{1,0:T(8,128)(2,1)S(1)}, bf16[8,8192]{1,0:T(8,128)(2,1)S(1)}, u32[]{:S(2)}, u32[]{:S(2)}) %collective-permute-start.2) | collective-permute-done | bytes 131104 | tf_op jit(solution)/shard_map/ppermute | solution.py:17
  29.8 0.0 collective-permute-start.3
  29.8 7.1 %collective-permute-done.3 = bf16[8,8192]{1,0:T(8,128)(2,1)S(1)} collective-permute-done((bf16[8,8192]{1,0:T(8,128)(2,1)S(1)}, bf16[8,8192]{1,0:T(8,128)(2,1)S(1)}, u32[]{:S(2)}, u32[]{:S(2)}) %collective-permute-start.3) | collective-permute-done | bytes 131104 | tf_op jit(solution)/shard_map/ppermute | solution.py:17
  36.9 0.0 collective-permute-start.4
  36.9 7.1 %collective-permute-done.4 = bf16[8,8192]{1,0:T(8,128)(2,1)S(1)} collective-permute-done((bf16[8,8192]{1,0:T(8,128)(2,1)S(1)}, bf16[8,8192]{1,0:T(8,128)(2,1)S(1)}, u32[]{:S(2)}, u32[]{:S(2)}) %collective-permute-start.4) | collective-permute-done | bytes 131104 | tf_op jit(solution)/shard_map/ppermute | solution.py:17
  44.0 0.0 collective-permute-start.5
  44.0 7.1 %collective-permute-done.5 = bf16[8,8192]{1,0:T(8,128)(2,1)S(1)} collective-permute-done((bf16[8,8192]{1,0:T(8,128)(2,1)S(1)}, bf16[8,8192]{1,0:T(8,128)(2,1)S(1)}, u32[]{:S(2)}, u32[]{:S(2)}) %collective-permute-start.5) | collective-permute-done | bytes 131104 | tf_op jit(solution)/shard_map/ppermute | solution.py:17
  51.1 0.0 collective-permute-start.6
  51.1 7.1 %collective-permute-done.6 = bf16[8,8192]{1,0:T(8,128)(2,1)S(1)} collective-permute-done((bf16[8,8192]{1,0:T(8,128)(2,1)S(1)}, bf16[8,8192]{1,0:T(8,128)(2,1)S(1)}, u32[]{:S(2)}, u32[]{:S(2)}) %collective-permute-start.6) | collective-permute-done | bytes 131104 | tf_op jit(solution)/shard_map/ppermute | solution.py:17
  58.2 0.0 collective-permute-start.7
  58.2 7.1 %collective-permute-done.7 = bf16[8,8192]{1,0:T(8,128)(2,1)S(1)} collective-permute-done((bf16[8,8192]{1,0:T(8,128)(2,1)S(1)}, bf16[8,8192]{1,0:T(8,128)(2,1)S(1)}, u32[]{:S(2)}, u32[]{:S(2)}) %collective-permute-start.7) | collective-permute-done | bytes 131104 | tf_op jit(solution)/shard_map/ppermute | solution.py:17
  65.2 0.0 collective-permute-start.8
  65.2 7.1 %collective-permute-done.8 = bf16[8,8192]{1,0:T(8,128)(2,1)S(1)} collective-permute-done((bf16[8,8192]{1,0:T(8,128)(2,1)S(1)}, bf16[8,8192]{1,0:T(8,128)(2,1)S(1)}, u32[]{:S(2)}, u32[]{:S(2)}) %collective-permute-start.8) | collective-permute-done | bytes 131104 | tf_op jit(solution)/shard_map/ppermute | solution.py:17
  72.3 0.0 collective-permute-start.9
  72.3 7.1 %collective-permute-done.9 = bf16[8,8192]{1,0:T(8,128)(2,1)S(1)} collective-permute-done((bf16[8,8192]{1,0:T(8,128)(2,1)S(1)}, bf16[8,8192]{1,0:T(8,128)(2,1)S(1)}, u32[]{:S(2)}, u32[]{:S(2)}) %collective-permute-start.9) | collective-permute-done | bytes 131104 | tf_op jit(solution)/shard_map/ppermute | solution.py:17
  79.4 0.0 collective-permute-start.10
  79.4 7.1 %collective-permute-done.10 = bf16[8,8192]{1,0:T(8,128)(2,1)S(1)} collective-permute-done((bf16[8,8192]{1,0:T(8,128)(2,1)S(1)}, bf16[8,8192]{1,0:T(8,128)(2,1)S(1)}, u32[]{:S(2)}, u32[]{:S(2)}) %collective-permute-start.10) | collective-permute-done | bytes 131104 | tf_op jit(solution)/shard_map/ppermute | solution.py:17
  86.5 0.0 collective-permute-start.11
  86.5 7.1 %collective-permute-done.11 = bf16[8,8192]{1,0:T(8,128)(2,1)S(1)} collective-permute-done((bf16[8,8192]{1,0:T(8,128)(2,1)S(1)}, bf16[8,8192]{1,0:T(8,128)(2,1)S(1)}, u32[]{:S(2)}, u32[]{:S(2)}) %collective-permute-start.11) | collective-permute-done | bytes 131104 | tf_op jit(solution)/shard_map/ppermute | solution.py:17
  93.6 0.0 collective-permute-start.12
  93.6 7.1 %collective-permute-done.12 = bf16[8,8192]{1,0:T(8,128)(2,1)S(1)} collective-permute-done((bf16[8,8192]{1,0:T(8,128)(2,1)S(1)}, bf16[8,8192]{1,0:T(8,128)(2,1)S(1)}, u32[]{:S(2)}, u32[]{:S(2)}) %collective-permute-start.12) | collective-permute-done | bytes 131104 | tf_op jit(solution)/shard_map/ppermute | solution.py:17
  100.7 0.0 collective-permute-start.13
  100.7 7.1 %collective-permute-done.13 = bf16[8,8192]{1,0:T(8,128)(2,1)S(1)} collective-permute-done((bf16[8,8192]{1,0:T(8,128)(2,1)S(1)}, bf16[8,8192]{1,0:T(8,128)(2,1)S(1)}, u32[]{:S(2)}, u32[]{:S(2)}) %collective-permute-start.13) | collective-permute-done | bytes 131104 | tf_op jit(solution)/shard_map/ppermute | solution.py:17
  107.8 0.0 collective-permute-start.14
  107.8 7.1 %collective-permute-done.14 = bf16[8,8192]{1,0:T(8,128)(2,1)S(1)} collective-permute-done((bf16[8,8192]{1,0:T(8,128)(2,1)S(1)}, bf16[8,8192]{1,0:T(8,128)(2,1)S(1)}, u32[]{:S(2)}, u32[]{:S(2)}) %collective-permute-start.14) | collective-permute-done | bytes 131104 | tf_op jit(solution)/shard_map/ppermute | solution.py:17
  115.0 0.0 copy-start.1
  115.2 0.9 constant_dynamic-update-slice_fusion.16
  116.4 0.0 copy-done
  116.4 0.5 fusion.8
  116.9 0.0 copy-done.1
  116.9 0.0 copy-start.2
  116.9 0.0 copy-start.3
  116.9 14.1 %convolution_convert_fusion = bf16[128,2004]{0,1:T(8,128)(2,1)S(1)} fusion(bf16[8192,2004]{0,1:T(8,128)(2,1)} %param.8, f32[8192]{0:T(1024)S(1)} %copy-done.1, bf16[256,8192]{1,0:T(8,128)(2,1)S(1)} %constant_dynamic-update-slice_fusion, s32[]{:T(128)S(6)} %select_n.37), kind=kOutput, calls=%fused_computation.14 | convolution fusion | flops 4206094848 | bytes 35476484 | tf_op jit(solution)/shard_map/dot_general | solution.py:56
  131.0 1.0 copy.8
  132.1 0.0 reduce-scatter.4.cloned.1.call-update
  132.1 0.0 copy-done.2
  132.1 0.1 dynamic_slice.50
  132.2 0.0 copy-done.3
  132.2 0.7 dynamic-slice
  133.6 11.0 %reduce-scatter.4.cloned.1.call-done = bf16[64,2005]{1,0:T(8,128)(2,1)} async-done(((bf16[128,2005]{1,0:T(8,128)(2,1)}), bf16[64,2005]{1,0:T(8,128)(2,1)}) %reduce-scatter.4.cloned.1.call-update) | async-done | bytes 256656
  144.6 1.2 copy.9
  145.8 0.1 convert_element_type.12
  145.9 0.3 fusion.13
  146.2 1.0 select_reduce_fusion
  147.2 0.2 dynamic-update-slice
  147.4 0.2 dynamic-update-slice.2
  147.7 0.2 dynamic-update-slice.1
  147.9 61.0 %all-reduce.3 = (f32[1024]{0:T(1024)S(1)}, f32[1024]{0:T(1024)S(1)}, f32[1024]{0:T(1024)S(1)}) all-reduce(f32[1024]{0:T(1024)S(1)} %dynamic-update-slice, f32[1024]{0:T(1024)S(1)} %dynamic-update-slice.1, f32[1024]{0:T(1024)S(1)} %dynamic-update-slice.2), channel_id=2, replica_groups=mesh['ha'=2,'vert'=16] {'vert'}, use_global_device_ids=true, to_apply=%add | all-reduce | flops 3072 | bytes 24576
  208.9 0.1 reshape.12
  209.0 0.1 reshape.13
  209.0 0.1 reshape.14
  209.1 0.7 while.19
  209.8 0.5 fusion.19
  210.3 0.1 fusion.12
  210.4 1.1 copy.7
  (55 shorter events, 0.8 us)
Async XLA Ops:
  7.2 109.2 %copy-start = (bf16[8,8192]{1,0:T(8,128)(2,1)S(1)}, bf16[8,8192]{1,0:T(8,128)(2,1)}, u32[]{:S(2)}) copy-start(bf16[8,8192]{1,0:T(8,128)(2,1)} %param.6) | copy-start | bytes 393220
  7.2 137.4 %reduce-scatter.4.cloned.1.call-start = ((), (), s32[]{:S(2)}) async-start(), calls=%async_computation.1 | async-start | bytes 786432
  7.2 8.4 %collective-permute-start = (bf16[8,8192]{1,0:T(8,128)(2,1)}, bf16[8,8192]{1,0:T(8,128)(2,1)S(1)}, u32[]{:S(2)}, u32[]{:S(2)}) collective-permute-start(bf16[8,8192]{1,0:T(8,128)(2,1)} %param.6), channel_id=1, source_target_pairs={{0,1},{1,2},{2,3},{3,4},{4,5},{5,6},{6,7},{7,8},{8,9},{9,10},{10,1... | collective-permute-start | bytes 393224 | tf_op jit(solution)/shard_map/ppermute | solution.py:17
  15.6 7.1 %collective-permute-start.1 = (bf16[8,8192]{1,0:T(8,128)(2,1)S(1)}, bf16[8,8192]{1,0:T(8,128)(2,1)S(1)}, u32[]{:S(2)}, u32[]{:S(2)}) collective-permute-start(bf16[8,8192]{1,0:T(8,128)(2,1)S(1)} %collective-permute-done), channel_id=1, source_target_pairs={{0,1},{1,2},{2,3},{3,4},{4,5},{5,6},{6,7},{7,8},{8,9},{9,10},{10,1... | collective-permute-start | bytes 393224 | tf_op jit(solution)/shard_map/ppermute | solution.py:17
  22.7 7.1 %collective-permute-start.2 = (bf16[8,8192]{1,0:T(8,128)(2,1)S(1)}, bf16[8,8192]{1,0:T(8,128)(2,1)S(1)}, u32[]{:S(2)}, u32[]{:S(2)}) collective-permute-start(bf16[8,8192]{1,0:T(8,128)(2,1)S(1)} %collective-permute-done.1), channel_id=1, source_target_pairs={{0,1},{1,2},{2,3},{3,4},{4,5},{5,6},{6,7},{7,8},{8,9},{9,10},{10,1... | collective-permute-start | bytes 393224 | tf_op jit(solution)/shard_map/ppermute | solution.py:17
  29.8 7.1 %collective-permute-start.3 = (bf16[8,8192]{1,0:T(8,128)(2,1)S(1)}, bf16[8,8192]{1,0:T(8,128)(2,1)S(1)}, u32[]{:S(2)}, u32[]{:S(2)}) collective-permute-start(bf16[8,8192]{1,0:T(8,128)(2,1)S(1)} %collective-permute-done.2), channel_id=1, source_target_pairs={{0,1},{1,2},{2,3},{3,4},{4,5},{5,6},{6,7},{7,8},{8,9},{9,10},{10,1... | collective-permute-start | bytes 393224 | tf_op jit(solution)/shard_map/ppermute | solution.py:17
  36.9 7.1 %collective-permute-start.4 = (bf16[8,8192]{1,0:T(8,128)(2,1)S(1)}, bf16[8,8192]{1,0:T(8,128)(2,1)S(1)}, u32[]{:S(2)}, u32[]{:S(2)}) collective-permute-start(bf16[8,8192]{1,0:T(8,128)(2,1)S(1)} %collective-permute-done.3), channel_id=1, source_target_pairs={{0,1},{1,2},{2,3},{3,4},{4,5},{5,6},{6,7},{7,8},{8,9},{9,10},{10,1... | collective-permute-start | bytes 393224 | tf_op jit(solution)/shard_map/ppermute | solution.py:17
  44.0 7.1 %collective-permute-start.5 = (bf16[8,8192]{1,0:T(8,128)(2,1)S(1)}, bf16[8,8192]{1,0:T(8,128)(2,1)S(1)}, u32[]{:S(2)}, u32[]{:S(2)}) collective-permute-start(bf16[8,8192]{1,0:T(8,128)(2,1)S(1)} %collective-permute-done.4), channel_id=1, source_target_pairs={{0,1},{1,2},{2,3},{3,4},{4,5},{5,6},{6,7},{7,8},{8,9},{9,10},{10,1... | collective-permute-start | bytes 393224 | tf_op jit(solution)/shard_map/ppermute | solution.py:17
  51.1 7.1 %collective-permute-start.6 = (bf16[8,8192]{1,0:T(8,128)(2,1)S(1)}, bf16[8,8192]{1,0:T(8,128)(2,1)S(1)}, u32[]{:S(2)}, u32[]{:S(2)}) collective-permute-start(bf16[8,8192]{1,0:T(8,128)(2,1)S(1)} %collective-permute-done.5), channel_id=1, source_target_pairs={{0,1},{1,2},{2,3},{3,4},{4,5},{5,6},{6,7},{7,8},{8,9},{9,10},{10,1... | collective-permute-start | bytes 393224 | tf_op jit(solution)/shard_map/ppermute | solution.py:17
  58.2 7.1 %collective-permute-start.7 = (bf16[8,8192]{1,0:T(8,128)(2,1)S(1)}, bf16[8,8192]{1,0:T(8,128)(2,1)S(1)}, u32[]{:S(2)}, u32[]{:S(2)}) collective-permute-start(bf16[8,8192]{1,0:T(8,128)(2,1)S(1)} %collective-permute-done.6), channel_id=1, source_target_pairs={{0,1},{1,2},{2,3},{3,4},{4,5},{5,6},{6,7},{7,8},{8,9},{9,10},{10,1... | collective-permute-start | bytes 393224 | tf_op jit(solution)/shard_map/ppermute | solution.py:17
  65.2 7.1 %collective-permute-start.8 = (bf16[8,8192]{1,0:T(8,128)(2,1)S(1)}, bf16[8,8192]{1,0:T(8,128)(2,1)S(1)}, u32[]{:S(2)}, u32[]{:S(2)}) collective-permute-start(bf16[8,8192]{1,0:T(8,128)(2,1)S(1)} %collective-permute-done.7), channel_id=1, source_target_pairs={{0,1},{1,2},{2,3},{3,4},{4,5},{5,6},{6,7},{7,8},{8,9},{9,10},{10,1... | collective-permute-start | bytes 393224 | tf_op jit(solution)/shard_map/ppermute | solution.py:17
  72.3 7.1 %collective-permute-start.9 = (bf16[8,8192]{1,0:T(8,128)(2,1)S(1)}, bf16[8,8192]{1,0:T(8,128)(2,1)S(1)}, u32[]{:S(2)}, u32[]{:S(2)}) collective-permute-start(bf16[8,8192]{1,0:T(8,128)(2,1)S(1)} %collective-permute-done.8), channel_id=1, source_target_pairs={{0,1},{1,2},{2,3},{3,4},{4,5},{5,6},{6,7},{7,8},{8,9},{9,10},{10,1... | collective-permute-start | bytes 393224 | tf_op jit(solution)/shard_map/ppermute | solution.py:17
  79.4 7.1 %collective-permute-start.10 = (bf16[8,8192]{1,0:T(8,128)(2,1)S(1)}, bf16[8,8192]{1,0:T(8,128)(2,1)S(1)}, u32[]{:S(2)}, u32[]{:S(2)}) collective-permute-start(bf16[8,8192]{1,0:T(8,128)(2,1)S(1)} %collective-permute-done.9), channel_id=1, source_target_pairs={{0,1},{1,2},{2,3},{3,4},{4,5},{5,6},{6,7},{7,8},{8,9},{9,10},{10,1... | collective-permute-start | bytes 393224 | tf_op jit(solution)/shard_map/ppermute | solution.py:17
  86.5 7.1 %collective-permute-start.11 = (bf16[8,8192]{1,0:T(8,128)(2,1)S(1)}, bf16[8,8192]{1,0:T(8,128)(2,1)S(1)}, u32[]{:S(2)}, u32[]{:S(2)}) collective-permute-start(bf16[8,8192]{1,0:T(8,128)(2,1)S(1)} %collective-permute-done.10), channel_id=1, source_target_pairs={{0,1},{1,2},{2,3},{3,4},{4,5},{5,6},{6,7},{7,8},{8,9},{9,10},{10,1... | collective-permute-start | bytes 393224 | tf_op jit(solution)/shard_map/ppermute | solution.py:17
  93.6 7.1 %collective-permute-start.12 = (bf16[8,8192]{1,0:T(8,128)(2,1)S(1)}, bf16[8,8192]{1,0:T(8,128)(2,1)S(1)}, u32[]{:S(2)}, u32[]{:S(2)}) collective-permute-start(bf16[8,8192]{1,0:T(8,128)(2,1)S(1)} %collective-permute-done.11), channel_id=1, source_target_pairs={{0,1},{1,2},{2,3},{3,4},{4,5},{5,6},{6,7},{7,8},{8,9},{9,10},{10,1... | collective-permute-start | bytes 393224 | tf_op jit(solution)/shard_map/ppermute | solution.py:17
  100.7 7.1 %collective-permute-start.13 = (bf16[8,8192]{1,0:T(8,128)(2,1)S(1)}, bf16[8,8192]{1,0:T(8,128)(2,1)S(1)}, u32[]{:S(2)}, u32[]{:S(2)}) collective-permute-start(bf16[8,8192]{1,0:T(8,128)(2,1)S(1)} %collective-permute-done.12), channel_id=1, source_target_pairs={{0,1},{1,2},{2,3},{3,4},{4,5},{5,6},{6,7},{7,8},{8,9},{9,10},{10,1... | collective-permute-start | bytes 393224 | tf_op jit(solution)/shard_map/ppermute | solution.py:17
  107.8 7.1 %collective-permute-start.14 = (bf16[8,8192]{1,0:T(8,128)(2,1)S(1)}, bf16[8,8192]{1,0:T(8,128)(2,1)S(1)}, u32[]{:S(2)}, u32[]{:S(2)}) collective-permute-start(bf16[8,8192]{1,0:T(8,128)(2,1)S(1)} %collective-permute-done.13), channel_id=1, source_target_pairs={{0,1},{1,2},{2,3},{3,4},{4,5},{5,6},{6,7},{7,8},{8,9},{9,10},{10,1... | collective-permute-start | bytes 393224 | tf_op jit(solution)/shard_map/ppermute | solution.py:17
  115.0 1.9 copy-start.1
  116.9 15.2 %copy-start.2 = (s32[128]{0:T(128)S(1)}, s32[128]{0:T(128)}, u32[]{:S(2)}) copy-start(s32[128]{0:T(128)} %param.9) | copy-start | bytes 1540
  116.9 15.3 %copy-start.3 = (u32[32]{0:T(128)S(1)}, u32[32]{0:T(128)}, u32[]{:S(2)}) copy-start(u32[32]{0:T(128)} %constant.102) | copy-start | bytes 388
Sparse Core Ops, SparseCore 0:
  132.2 12.3 reduce-scatter.3
